TPU v7x, 32 devices: a whole 2x2x4 slice. The times are simulated.
32 devices in a mesh: grp: 4 (over y, core), dp: 8 (over z, x).
Axes of the slice: x: 2, y: 2, z: 4, core: 2. Of those that a mesh axis runs over, the one named last changes fastest.
Arguments:
- tokens: bfloat16 [4, 1024, 2048], P('grp', 'dp'), may hold values from -6 to 6
- hidden_grad: bfloat16 [4, 1024, 6144], P('grp', 'dp'), may hold values from -6 to 6
- w_gate: bfloat16 [4, 2048, 6144], P('grp', None, 'dp'), may hold values from -6 to 6
- w_up: bfloat16 [4, 2048, 6144], P('grp', None, 'dp'), may hold values from -6 to 6
Outputs:
- mixed_gate: bfloat16 [4, 2048, 6144], P('grp', None, 'dp')
- mixed_up: bfloat16 [4, 2048, 6144], P('grp', None, 'dp')
All inputs are finite; a program needn't handle non-finite values.
Results may differ from a plain program's by a relative error of at most 0.0052.
Values may be sent and summed in bfloat16 or wider, within the bound.
A program may use at most 256 MiB of HBM per device.

v0:
```python
import functools
import math

import jax
import jax.numpy as jnp
from jax import lax
from jax.experimental import pallas as pl
from jax.experimental.pallas import tpu as pltpu
from jax.sharding import PartitionSpec as P

LANES = 128
BLOCK = 256
VMEM = pl.BlockSpec(memory_space=pltpu.VMEM)
ANY = pl.BlockSpec(memory_space=pl.ANY)
MESH = pl.DeviceIdType.MESH
F32, BF16 = jnp.float32, jnp.bfloat16


def inner_size(n):
    return max(d for d in range(1, n + 1) if n % d == 0 and d * d <= n)


def early_units(units):
    return max(units // 3 // LANES, 1) * LANES


def aligned(index, size):
    return pl.ds(pl.multiple_of(index * size, size), size)


def kernel(n, groups, cut, *refs):
    tokens, hidden, w_gate, w_up, out_gate, out_up = refs[:6]
    tok, tok_t, cot, held, near, far, far_tok, far_tok_t, far_cot, gate_rows, up_rows = refs[6:17]
    local_sem, gather_sems, far_gather_sems, cot_sems, early_sems, early_cot_sems, near_sems, far_sems = (
        refs[17:18] + (refs[18:24], refs[24:30], refs[30:32], refs[32:34], refs[34:36], refs[36:38], refs[38:40])
    )
    nx = inner_size(n)
    nz = n // nx
    rows, depth = tokens.shape
    units = w_gate.shape[1]
    scale = depth ** (-0.5)
    blocks = depth // BLOCK
    grp, me = lax.axis_index("grp"), lax.axis_index("dp")
    z, x = me // nx, lax.rem(me, nx)
    odd = lax.rem(grp, 2) == 1
    near_grp = jnp.where(odd, grp - 1, grp + 1)
    far_grp = jnp.where(odd, lax.rem(grp + 1, groups), lax.rem(grp + groups - 1, groups))

    mine = pltpu.make_async_copy(tokens, tok.at[aligned(me, rows), :], local_sem.at[0])
    mine.start()
    own_cot = pltpu.make_async_copy(
        hidden.at[:, aligned(me, units)], cot.at[aligned(me, rows), :], local_sem.at[1]
    )
    own_cot.start()
    weights = [pltpu.make_async_copy(w, held.at[s], local_sem.at[2 + s]) for s, w in enumerate((w_gate, w_up))]
    for copy in weights:
        copy.start()

    barrier = pltpu.get_barrier_semaphore()
    for j in range(1, n):
        pl.semaphore_signal(barrier, inc=1, device_id={"dp": lax.rem(me + j, n)}, device_id_type=MESH)
    pl.semaphore_signal(barrier, inc=1, device_id={"grp": near_grp}, device_id_type=MESH)
    for j in range(n):
        pl.semaphore_signal(barrier, inc=1, device_id={"grp": far_grp, "dp": j}, device_id_type=MESH)
    pl.semaphore_wait(barrier, 2 * n)

    def remote(src, dst, send, recv, **to):
        return pltpu.make_async_remote_copy(
            src_ref=src, dst_ref=dst, send_sem=send, recv_sem=recv, device_id=to, device_id_type=MESH
        )

    def early_tokens():
        return remote(tokens, far_tok.at[aligned(me, rows), :], early_sems[0].at[0], early_sems[1].at[0], grp=far_grp)

    def early_weights(s):
        return remote(
            (w_gate, w_up)[s].at[:, :cut], far.at[s, :, :cut],
            early_sems[0].at[1 + s], early_sems[1].at[1 + s], grp=far_grp,
        )

    def early_cot(j):
        return remote(
            hidden.at[:, pl.ds(j * units, cut)], far_cot.at[aligned(me, rows), :],
            early_cot_sems[0].at[j], early_cot_sems[1].at[me], grp=far_grp, dp=j,
        )

    def early_cot_arrival(source):
        place = far_cot.at[aligned(source, rows), :]
        return remote(place, place, early_cot_sems[0].at[source], early_cot_sems[1].at[source], grp=far_grp, dp=source)

    @pl.when(odd)
    def _():
        early_tokens().start()
        for s in range(2):
            early_weights(s).start()
        early_weights(0).wait_send()
        for j in range(n):
            early_cot(j).start()
        early_weights(1).wait_send()

    def cot_send(zz, xx):
        to = zz * nx + xx
        return remote(
            hidden.at[:, aligned(to, units)], cot.at[aligned(me, rows), :], cot_sems[0].at[to], cot_sems[1].at[me], dp=to
        )

    def cot_arrival(source):
        place = cot.at[aligned(source, rows), :]
        return remote(place, place, cot_sems[0].at[source], cot_sems[1].at[source], dp=source)

    def collect(buf, turned, cot_buf, weight, gate_out, up_out, sems, send_cot, wait_cot):
        up_send, up_recv, down_send, down_recv, side_send, side_recv = sems

        def slot(zz, xx):
            return buf.at[aligned(zz * nx + xx, rows), :]

        def up(zz):
            return remote(slot(zz, x), slot(zz, x), up_send.at[zz], up_recv.at[zz], dp=(z + 1) * nx + x)

        def up_arrival(zz):
            return remote(slot(zz, x), slot(zz, x), up_send.at[zz], up_recv.at[zz], dp=(z - 1) * nx + x)

        def down(zz):
            return remote(slot(zz, x), slot(zz, x), down_send.at[zz], down_recv.at[zz], dp=(z - 1) * nx + x)

        def down_arrival(zz):
            return remote(slot(zz, x), slot(zz, x), down_send.at[zz], down_recv.at[zz], dp=(z + 1) * nx + x)

        def side(zz, j):
            return remote(
                slot(zz, x), slot(zz, x), side_send.at[zz, j - 1], side_recv.at[zz, j - 1],
                dp=z * nx + lax.rem(x + j, nx),
            )

        def side_arrival(zz, j):
            other = lax.rem(x + nx - j, nx)
            return remote(
                slot(zz, other), slot(zz, other), side_send.at[zz, j - 1], side_recv.at[zz, j - 1], dp=z * nx + other
            )

        def forward_on(zz):
            pl.when(z + 1 < nz)(lambda: up(zz).start())

        def backward_on(zz):
            pl.when(z >= 1)(lambda: down(zz).start())

        forward_on(z)
        backward_on(z)
        for j in range(1, nx):
            side(z, j).start()
        send_cot(0)
        span = nx * rows
        least = jnp.minimum(z, nz - 1 - z)
        longer = jnp.where(z < nz - 1 - z, 1, -1)

        @pl.loop(0, nz)
        def _(r):
            @pl.when((r < nz - 1) & (z - 1 - r >= 0))
            def _():
                zz = z - 1 - r
                up_arrival(zz).wait_recv()
                forward_on(zz)
                for j in range(1, nx):
                    side(zz, j).start()

            @pl.when((r < nz - 1) & (z + 1 + r < nz))
            def _():
                zz = z + 1 + r
                down_arrival(zz).wait_recv()
                backward_on(zz)
                for j in range(1, nx):
                    side(zz, j).start()

            pl.when(r < nz - 1)(lambda: send_cot(r + 1))

            near_turn = r <= 2 * least
            step = jnp.where(near_turn, (r + 1) // 2, r - least)
            sign = jnp.where(near_turn, jnp.where(lax.rem(r, 2) == 1, -1, 1), longer)
            zz = z + sign * step
            for j in range(1, nx):
                side_arrival(zz, j).wait_recv()
            for xx in range(nx):
                wait_cot(zz * nx + xx)
            part = aligned(zz, span)
            block = buf[part, :]
            turned[:, part] = block.T
            gate = jnp.dot(block, weight(0), preferred_element_type=F32) * scale
            up_value = jnp.dot(block, weight(1), preferred_element_type=F32) * scale
            sigma = jax.nn.sigmoid(gate)
            upstream = cot_buf[part, :].astype(F32)
            gate_out(part, (upstream * up_value * sigma * (1.0 + gate * (1.0 - sigma))).astype(BF16))
            up_out(part, (upstream * gate * sigma).astype(BF16))

        def settle():
            @pl.loop(0, nz)
            def _(zz):
                for j in range(1, nx):
                    side(zz, j).wait_send()
                pl.when((z + 1 < nz) & (zz <= z))(lambda: up(zz).wait_send())
                pl.when((z >= 1) & (zz >= z))(lambda: down(zz).wait_send())

        return settle

    def send_cot(d):
        def to_row(zz):
            for xx in range(nx):
                pl.when(zz * nx + xx != me)(lambda: cot_send(zz, xx).start())

        if isinstance(d, int) and d == 0:
            to_row(z)
        else:
            pl.when(z - d >= 0)(lambda: to_row(z - d))
            pl.when(z + d < nz)(lambda: to_row(z + d))

    def wait_cot(source):
        pl.when(source != me)(lambda: cot_arrival(source).wait_recv())

    mine.wait()
    own_cot.wait()
    for copy in weights:
        copy.wait()

    def put(ref, width):
        def store(part, value):
            ref[part, :width] = value

        return store

    settle_own = collect(
        tok, tok_t, cot, lambda s: held[s], put(gate_rows, units), put(up_rows, units), gather_sems, send_cot, wait_cot
    )

    def near_copy(i):
        place = (slice(None), aligned(i, BLOCK), slice(None))
        return remote(held.at[place], near.at[place], near_sems[0].at[i], near_sems[1].at[i], grp=near_grp)

    def far_copy(i, whole):
        place = (slice(None), aligned(i, BLOCK), slice(None) if whole else pl.ds(cut, units - cut))
        return remote(held.at[place], far.at[place], far_sems[0].at[i], far_sems[1].at[i], grp=far_grp)

    def send_steps(i):
        pl.when(odd)(lambda: far_copy(i, False).start())
        pl.when(jnp.logical_not(odd))(lambda: far_copy(i, True).start())
        near_copy(i).start()

    @pl.loop(0, blocks)
    def _(i):
        part = aligned(i, BLOCK)
        turned = tok_t[part, :]
        for s, unit_rows in enumerate((gate_rows, up_rows)):
            gradient = jnp.dot(turned, unit_rows[...], preferred_element_type=F32) * scale
            held[s, part, :] = (held[s, part, :].astype(F32) - 0.5 * gradient).astype(BF16)
        pl.when(i >= 1)(lambda: send_steps(i - 1))

    send_steps(blocks - 1)

    @pl.when(jnp.logical_not(odd))
    def _():
        near_copy(0).wait_recv()
        early_tokens().wait_recv()
        for s in range(2):
            early_weights(s).wait_recv()
        settle_far = collect(
            far_tok, far_tok_t, far_cot, lambda s: far[s, :, :cut], put(gate_rows, cut), put(up_rows, cut),
            far_gather_sems, lambda d: None, lambda source: early_cot_arrival(source).wait_recv(),
        )

        @pl.loop(0, blocks)
        def _(i):
            part = aligned(i, BLOCK)
            turned = far_tok_t[part, :]
            for s, unit_rows in enumerate((gate_rows, up_rows)):
                gradient = jnp.dot(turned, unit_rows[:, :cut], preferred_element_type=F32) * scale
                far[s, part, :cut] = (far[s, part, :cut].astype(F32) - 0.5 * gradient).astype(BF16)

        settle_far()

    @pl.loop(0, blocks)
    def _(i):
        @pl.when(odd)
        def _():
            near_copy(i).wait_recv()
            far_copy(i, True).wait_recv()

        @pl.when(jnp.logical_not(odd))
        def _():
            pl.when(i >= 1)(lambda: near_copy(i).wait_recv())
            far_copy(i, False).wait_recv()

        part = aligned(i, BLOCK)
        for s, out in enumerate((out_gate, out_up)):
            mixed = 0.5 * held[s, part, :].astype(F32) + 0.25 * (
                near[s, part, :].astype(F32) + far[s, part, :].astype(F32)
            )
            out[part, :] = mixed.astype(BF16)

    settle_own()

    @pl.loop(0, n)
    def _(j):
        pl.when(j != me)(lambda: cot_arrival(j).wait_send())

    @pl.when(odd)
    def _():
        early_tokens().wait_send()
        for j in range(n):
            early_cot(j).wait_send()

    @pl.loop(0, blocks)
    def _(i):
        near_copy(i).wait_send()
        pl.when(odd)(lambda: far_copy(i, False).wait_send())
        pl.when(jnp.logical_not(odd))(lambda: far_copy(i, True).wait_send())


def local(tokens, hidden_grad, w_gate, w_up):
    n, groups = lax.axis_size("dp"), lax.axis_size("grp")
    nx = inner_size(n)
    nz = n // nx
    tokens, hidden_grad, w_gate, w_up = tokens[0], hidden_grad[0], w_gate[0], w_up[0]
    rows, depth = tokens.shape
    units = w_gate.shape[1]
    total = n * rows
    cut = early_units(units)
    blocks = depth // BLOCK
    dma = pltpu.SemaphoreType.DMA
    hops = [dma((nz,))] * 4 + [dma((nz, max(nx - 1, 1)))] * 2
    scratch = [
        pltpu.VMEM((total, depth), BF16),
        pltpu.VMEM((depth, total), BF16),
        pltpu.VMEM((total, units), BF16),
        pltpu.VMEM((2, depth, units), BF16),
        pltpu.VMEM((2, depth, units), BF16),
        pltpu.VMEM((2, depth, units), BF16),
        pltpu.VMEM((total, depth), BF16),
        pltpu.VMEM((depth, total), BF16),
        pltpu.VMEM((total, cut), BF16),
        pltpu.VMEM((total, units), BF16),
        pltpu.VMEM((total, units), BF16),
        dma((4,)),
        *hops,
        *hops,
        dma((n,)), dma((n,)),
        dma((3,)), dma((3,)),
        dma((n,)), dma((n,)),
        dma((blocks,)), dma((blocks,)),
        dma((blocks,)), dma((blocks,)),
    ]
    shape = jax.ShapeDtypeStruct(w_gate.shape, w_gate.dtype)
    outs = pl.pallas_call(
        functools.partial(kernel, n, groups, cut),
        out_shape=[shape, shape],
        in_specs=[ANY] * 4,
        out_specs=[VMEM] * 2,
        scratch_shapes=scratch,
        compiler_params=pltpu.CompilerParams(
            collective_id=0, has_side_effects=True, vmem_limit_bytes=56 * 1024 * 1024
        ),
        name="gossip_step",
    )(tokens, hidden_grad, w_gate, w_up)
    return tuple(out[None] for out in outs)


def solution(mesh):
    in_specs = (
        P("grp", "dp", None),
        P("grp", "dp", None),
        P("grp", None, "dp"),
        P("grp", None, "dp"),
    )
    out_specs = (P("grp", None, "dp"), P("grp", None, "dp"))
    return jax.shard_map(local, mesh=mesh, in_specs=in_specs, out_specs=out_specs, check_vma=False)
```

profile of v0, /device:TPU:6, one launch (start us, length us, event | category | flops | bytes accessed | tf_op | source)
XLA Modules:
  0.0 183.0 jit_solution(12881571340045672837)
XLA Ops:
  0.6 176.8 %gossip_step.1 = (bf16[2048,768]{1,0:T(8,128)(2,1)}, bf16[2048,768]{1,0:T(8,128)(2,1)}) custom-call(bf16[128,2048]{1,0:T(8,128)(2,1)} %bitcast.11, bf16[128,6144]{1,0:T(8,128)(2,1)} %bitcast.10, bf16[2048,768]{1,0:T(8,128)(2,1)} %bitcast.8, bf16[2048,768]{1,0:T(8,128)(2,1)} %bitcast.9), custom_call_target="tpu_custom_call" | custom-call | tf_op jit(solution)/shard_map/gossip_step/pallas_call | solution.py:350
  177.4 0.0 copy-start
  177.4 3.9 %copy.8 = bf16[1,2048,768]{2,1,0:T(8,128)(2,1)} copy(bf16[1,2048,768]{2,1,0:T(8,128)(2,1)} %bitcast.7) | data formatting | bytes 6291456
  181.3 0.0 copy-done
  181.3 1.7 copy.9
Async XLA Ops:
  177.4 3.9 %copy-start = (bf16[2048,768]{1,0:T(8,128)(2,1)S(1)}, bf16[2048,768]{1,0:T(8,128)(2,1)}, u32[]{:S(2)}) copy-start(bf16[2048,768]{1,0:T(8,128)(2,1)} %get-tuple-element.5) | copy-start | bytes 9437188
where the time goes:
time: 183 us
  Pallas kernels  177 us (97%)
  local copies, waits for them, and re-layouts  5.57 us (3%)
    pallas_call x1, Pallas kernels, local(): pl.pallas_call(functools.partial(kernel, n, groups, cut), out_shape=[shap...  177 us
    unnamed x4, local copies, waits for them, and re-layouts  5.57 us

commit v1 on v0

v1 whole, which is shorter than its diff:
```python
import functools

import jax
import jax.numpy as jnp
from jax import lax
from jax.experimental import pallas as pl
from jax.experimental.pallas import tpu as pltpu
from jax.sharding import PartitionSpec as P

LANES = 128
BLOCK = 256
PIECES = 2
VMEM_LIMIT = 54 * 1024 * 1024
VMEM = pl.BlockSpec(memory_space=pltpu.VMEM)
ANY = pl.BlockSpec(memory_space=pl.ANY)
MESH = pl.DeviceIdType.MESH
F32, BF16 = jnp.float32, jnp.bfloat16


def inner_size(n):
    return max(d for d in range(1, n + 1) if n % d == 0 and d * d <= n)


def slab_count(units):
    return next(count for count in (3, 2, 1) if units % (count * LANES) == 0)


def aligned(index, size):
    return pl.ds(pl.multiple_of(index * size, size), size)


def kernel(n, groups, *refs):
    tokens, hidden, w_gate, w_up, far = refs[:5]
    tok, tok_t, cot, held, near, far_tok, far_tok_t, far_cot, stage, gate_rows, up_rows, gate_pre, up_pre = refs[5:18]
    local_sem, weight_sem, turn_sem = refs[18:21]
    gather_sems, far_gather_sems = refs[21:27], refs[27:33]
    cot_sems, far_cot_sems, early_sems, early_cot_sems, near_sems, far_sems = (
        refs[k : k + 2] for k in range(33, 45, 2)
    )
    nx = inner_size(n)
    nz = n // nx
    rows, depth = tokens.shape
    units = w_gate.shape[1]
    slabs, _, _, width = held.shape
    scale = depth ** (-0.5)
    blocks = depth // BLOCK
    span = nx * rows
    grp, me = lax.axis_index("grp"), lax.axis_index("dp")
    z, x = me // nx, lax.rem(me, nx)
    odd = lax.rem(grp, 2) == 1
    even = jnp.logical_not(odd)
    near_grp = jnp.where(odd, grp - 1, grp + 1)
    far_grp = jnp.where(odd, lax.rem(grp + 1, groups), lax.rem(grp + groups - 1, groups))

    def hidden_part(to, h):
        return hidden.at[:, pl.ds(pl.multiple_of(to * units + h * width, LANES), width)]

    mine = [pltpu.make_async_copy(tokens, tok.at[aligned(me, rows), :], local_sem.at[slabs])]
    for h in range(slabs):
        mine.append(pltpu.make_async_copy(hidden_part(me, h), cot.at[h, aligned(me, rows), :], local_sem.at[h]))
    for h in range(slabs):
        for s, w in enumerate((w_gate, w_up)):
            mine.append(
                pltpu.make_async_copy(w.at[:, pl.ds(h * width, width)], held.at[h, s], weight_sem.at[h, s])
            )
    for copy in mine:
        copy.start()

    with jax.named_scope("barrier"):
        barrier = pltpu.get_barrier_semaphore()

        def greet(**to):
            pl.semaphore_signal(barrier, inc=1, device_id=to, device_id_type=MESH)

        for j in range(1, nx):
            greet(dp=z * nx + lax.rem(x + j, nx))
        pl.when(z >= 1)(lambda: greet(dp=me - nx))
        pl.when(z + 1 < nz)(lambda: greet(dp=me + nx))
        greet(grp=near_grp)
        greet(grp=far_grp)
        pl.semaphore_wait(barrier, nx + 1 + jnp.where(z >= 1, 1, 0) + jnp.where(z + 1 < nz, 1, 0))

    def remote(src, dst, send, recv, **to):
        return pltpu.make_async_remote_copy(
            src_ref=src, dst_ref=dst, send_sem=send, recv_sem=recv, device_id=to, device_id_type=MESH
        )

    def early_tokens():
        return remote(tokens, far_tok.at[aligned(me, rows), :], early_sems[0].at[0], early_sems[1].at[0], grp=far_grp)

    def early_weights(s):
        return remote(
            (w_gate, w_up)[s].at[:, :width], far.at[0, s], early_sems[0].at[1 + s], early_sems[1].at[1 + s], grp=far_grp
        )

    def early_cot(j, own):
        place = far_cot.at[aligned(me, rows), :] if own else stage.at[:, aligned(j, width)]
        return remote(hidden_part(j, 0), place, early_cot_sems[0].at[j], early_cot_sems[1].at[j], grp=far_grp)

    def early():
        copies = [early_tokens(), early_weights(0), early_weights(1)]
        copies += [early_cot(lax.rem(me + j, n), False) for j in range(1, n)]
        return copies + [early_cot(me, True)]

    def relay(buf, sems):
        up_send, up_recv, down_send, down_recv, side_send, side_recv = sems
        piece = rows // PIECES

        def slot(zz, xx, c):
            return buf.at[aligned((zz * nx + xx) * PIECES + c, piece), :]

        def along(zz, c, pair, to):
            place = slot(zz, x, c)
            return remote(place, place, pair[0].at[zz, c], pair[1].at[zz, c], dp=to * nx + x)

        def up(zz, c, back=False):
            return along(zz, c, (up_send, up_recv), z - 1 if back else z + 1)

        def down(zz, c, back=False):
            return along(zz, c, (down_send, down_recv), z + 1 if back else z - 1)

        def side(zz, j, c):
            place = slot(zz, x, c)
            return remote(
                place, place, side_send.at[zz, j - 1, c], side_recv.at[zz, j - 1, c], dp=z * nx + lax.rem(x + j, nx)
            )

        def side_arrival(zz, j, c):
            other = lax.rem(x + nx - j, nx)
            place = slot(zz, other, c)
            return remote(place, place, side_send.at[zz, j - 1, c], side_recv.at[zz, j - 1, c], dp=z * nx + other)

        def pass_on(zz, c, upward):
            if upward is not False:
                pl.when(z + 1 < nz)(lambda: up(zz, c).start())
            if upward is not True:
                pl.when(z >= 1)(lambda: down(zz, c).start())
            for j in range(1, nx):
                side(zz, j, c).start()

        def begin():
            for c in range(PIECES):
                pass_on(z, c, None)

        def turn(r, then):
            for c in range(PIECES):
                @pl.when(z - 1 - r >= 0)
                def _():
                    with jax.named_scope("wait_up"):
                        up(z - 1 - r, c, True).wait_recv()
                    pass_on(z - 1 - r, c, True)

                @pl.when(z + 1 + r < nz)
                def _():
                    with jax.named_scope("wait_down"):
                        down(z + 1 + r, c, True).wait_recv()
                    pass_on(z + 1 + r, c, False)

            pl.when(z - 1 - r >= 0)(lambda: then(z - 1 - r))
            pl.when(z + 1 + r < nz)(lambda: then(z + 1 + r))

        def row_ready(zz):
            for j in range(1, nx):
                for c in range(PIECES):
                    side_arrival(zz, j, c).wait_recv()

        def settle():
            @pl.loop(0, nz)
            def _(zz):
                for c in range(PIECES):
                    for j in range(1, nx):
                        side(zz, j, c).wait_send()
                    pl.when((z + 1 < nz) & (zz <= z))(lambda: up(zz, c).wait_send())
                    pl.when((z >= 1) & (zz >= z))(lambda: down(zz, c).wait_send())

        return begin, turn, row_ready, settle

    def swap(block_of, buf_of, sems):
        def send(to, h):
            return remote(block_of(to, h), buf_of(h).at[aligned(me, rows), :], sems[0].at[h, to], sems[1].at[h, me], dp=to)

        def arrival(source, h):
            place = buf_of(h).at[aligned(source, rows), :]
            return remote(place, place, sems[0].at[h, source], sems[1].at[h, source], dp=source)

        def send_row(zz, h):
            for xx in range(nx):
                pl.when(zz * nx + xx != me)(lambda: send(zz * nx + xx, h).start())

        def row_ready(zz, h):
            for xx in range(nx):
                pl.when(zz * nx + xx != me)(lambda: arrival(zz * nx + xx, h).wait_recv())

        def settle(h):
            @pl.loop(0, n)
            def _(j):
                pl.when(j != me)(lambda: arrival(j, h).wait_send())

        return send_row, row_ready, settle

    least = jnp.minimum(z, nz - 1 - z)
    longer = jnp.where(z < nz - 1 - z, 1, -1)

    def arriving(r):
        near_turn = r <= 2 * least
        step = jnp.where(near_turn, (r + 1) // 2, r - least)
        sign = jnp.where(near_turn, jnp.where(lax.rem(r, 2) == 1, -1, 1), longer)
        return z + sign * step

    def turn_over(buf, turned, zz):
        turned[:, aligned(zz, span)] = buf[aligned(zz, span), :].T

    def project(buf, gate_weight, up_weight, zz):
        part = aligned(zz, span)
        block = buf[part, :]
        gate_pre[part, :] = jnp.dot(block, gate_weight, preferred_element_type=F32) * scale
        up_pre[part, :] = jnp.dot(block, up_weight, preferred_element_type=F32) * scale

    def activate(cotangent, zz):
        part = aligned(zz, span)
        gate = gate_pre[part, :]
        sigma = jax.nn.sigmoid(gate)
        upstream = cotangent[part, :].astype(F32)
        gate_rows[part, :] = (upstream * up_pre[part, :] * sigma * (1.0 + gate * (1.0 - sigma))).astype(BF16)
        up_rows[part, :] = (upstream * gate * sigma).astype(BF16)

    def update(turned, weight, h, i):
        part = aligned(i, BLOCK)
        block = turned[part, :]
        for s, unit_rows in enumerate((gate_rows, up_rows)):
            gradient = jnp.dot(block, unit_rows[...], preferred_element_type=F32) * scale
            weight[h, s, part, :] = (weight[h, s, part, :].astype(F32) - 0.5 * gradient).astype(BF16)

    def near_copy(h, i):
        place = (h, slice(None), aligned(i, BLOCK))
        return remote(held.at[place], near.at[place], near_sems[0].at[h, i], near_sems[1].at[h, i], grp=near_grp)

    def far_copy(h, i):
        place = (h, slice(None), aligned(i, BLOCK))
        return remote(held.at[place], far.at[place], far_sems[0].at[h, i], far_sems[1].at[h, i], grp=far_grp)

    def send_steps(h, i):
        pl.when(even | (h > 0))(lambda: far_copy(h, i).start())
        near_copy(h, i).start()

    @pl.when(odd)
    def _():
        for copy in early():
            copy.start()
        with jax.named_scope("wait_turn"):
            pl.semaphore_wait(turn_sem, 1)

    begin, turn, tokens_ready, settle_tokens = relay(tok, gather_sems)
    send_cot, cot_ready, settle_cot = swap(hidden_part, lambda h: cot.at[h], cot_sems)
    for copy in mine:
        copy.wait()
    begin()
    send_cot(z, 0)

    @pl.loop(0, nz)
    def _(r):
        pl.when(r < nz - 1)(lambda: turn(r, lambda zz: send_cot(zz, 0)))
        zz = arriving(r)
        with jax.named_scope("wait_side"):
            tokens_ready(zz)
        with jax.named_scope("project"):
            turn_over(tok, tok_t, zz)
            project(tok, held[0, 0], held[0, 1], zz)

    @pl.loop(1, slabs)
    def _(h):
        @pl.loop(0, nz)
        def _(r):
            send_cot(arriving(r), h)

    @pl.loop(0, slabs)
    def _(h):
        @pl.when(h > 0)
        def _():
            @pl.loop(0, nz)
            def _(zz):
                project(tok, held[h, 0], held[h, 1], zz)

        @pl.loop(0, nz)
        def _(r):
            zz = arriving(r)
            with jax.named_scope("wait_cot"):
                cot_ready(zz, h)
            with jax.named_scope("forward"):
                activate(cot.at[h], zz)

        @pl.when((h == slabs - 1) & even)
        def _():
            pl.semaphore_signal(turn_sem, inc=1, device_id={"grp": near_grp}, device_id_type=MESH)

        @pl.loop(0, blocks)
        def _(i):
            with jax.named_scope("step"):
                update(tok_t, held, h, i)
            pl.when(i >= 1)(lambda: send_steps(h, i - 1))

        send_steps(h, blocks - 1)

    @pl.when(even)
    def _():
        with jax.named_scope("wait_sibling"):
            near_copy(0, 0).wait_recv()
        for copy in early():
            copy.wait_recv()
        begin, turn, tokens_ready, settle_far_tokens = relay(far_tok, far_gather_sems)
        send_cot, cot_ready, settle_far_cot = swap(
            lambda to, h: stage.at[:, aligned(to, width)], lambda h: far_cot, far_cot_sems
        )
        begin()

        @pl.loop(0, nz)
        def _(r):
            send_cot(arriving(r), 0)

        @pl.loop(0, nz)
        def _(r):
            pl.when(r < nz - 1)(lambda: turn(r, lambda zz: None))
            zz = arriving(r)
            with jax.named_scope("wait_side"):
                tokens_ready(zz)
            with jax.named_scope("forward_far"):
                turn_over(far_tok, far_tok_t, zz)
                project(far_tok, far[0, 0], far[0, 1], zz)

        @pl.loop(0, nz)
        def _(zz):
            with jax.named_scope("wait_cot"):
                cot_ready(zz, 0)
            activate(far_cot, zz)

        @pl.loop(0, blocks)
        def _(i):
            with jax.named_scope("step_far"):
                update(far_tok_t, far, 0, i)

        settle_far_tokens()
        settle_far_cot(0)

    settle_tokens()
    for h in range(slabs):
        settle_cot(h)

    @pl.when(odd)
    def _():
        for copy in early():
            copy.wait_send()

    @pl.loop(0, slabs)
    def _(h):
        @pl.loop(0, blocks)
        def _(i):
            near_copy(h, i).wait_send()
            pl.when(even | (h > 0))(lambda: far_copy(h, i).wait_send())
            with jax.named_scope("wait_near"):
                pl.when(odd | (h > 0) | (i > 0))(lambda: near_copy(h, i).wait_recv())
            with jax.named_scope("wait_far"):
                pl.when(odd | (h > 0))(lambda: far_copy(h, i).wait_recv())
            with jax.named_scope("mix"):
                part = aligned(i, BLOCK)
                for s in range(2):
                    mixed = 0.5 * held[h, s, part, :].astype(F32) + 0.25 * (
                        near[h, s, part, :].astype(F32) + far[h, s, part, :].astype(F32)
                    )
                    far[h, s, part, :] = mixed.astype(BF16)


def place_kernel(mixed, out_gate, out_up, sems):
    slabs, _, _, width = mixed.shape
    copies = [
        pltpu.make_async_copy(mixed.at[h, s], out.at[:, pl.ds(h * width, width)], sems.at[h, s])
        for h in range(slabs)
        for s, out in enumerate((out_gate, out_up))
    ]
    for copy in copies:
        copy.start()
    for copy in copies:
        copy.wait()


def local(tokens, hidden_grad, w_gate, w_up):
    n, groups = lax.axis_size("dp"), lax.axis_size("grp")
    nx = inner_size(n)
    nz = n // nx
    args = [pltpu.with_memory_space_constraint(a[0], pltpu.HBM) for a in (tokens, hidden_grad, w_gate, w_up)]
    rows, depth = args[0].shape
    units = args[2].shape[1]
    total = n * rows
    slabs = slab_count(units)
    width = units // slabs
    blocks = depth // BLOCK
    dma = pltpu.SemaphoreType.DMA
    hops = [dma((nz, PIECES))] * 4 + [dma((nz, max(nx - 1, 1), PIECES))] * 2
    weights = (slabs, 2, depth, width)
    scratch = [
        pltpu.VMEM((total, depth), BF16),
        pltpu.VMEM((depth, total), BF16),
        pltpu.VMEM((slabs, total, width), BF16),
        pltpu.VMEM(weights, BF16),
        pltpu.VMEM(weights, BF16),
        pltpu.VMEM((total, depth), BF16),
        pltpu.VMEM((depth, total), BF16),
        pltpu.VMEM((total, width), BF16),
        pltpu.VMEM((rows, n * width), BF16),
        pltpu.VMEM((total, width), BF16),
        pltpu.VMEM((total, width), BF16),
        pltpu.VMEM((total, width), F32),
        pltpu.VMEM((total, width), F32),
        dma((slabs + 1,)), dma((slabs, 2)), pltpu.SemaphoreType.REGULAR,
        *hops,
        *hops,
        dma((slabs, n)), dma((slabs, n)),
        dma((1, n)), dma((1, n)),
        dma((3,)), dma((3,)),
        dma((n,)), dma((n,)),
        dma((slabs, blocks)), dma((slabs, blocks)),
        dma((slabs, blocks)), dma((slabs, blocks)),
    ]
    mixed = pl.pallas_call(
        functools.partial(kernel, n, groups),
        out_shape=pltpu.VMEM(weights, BF16),
        in_specs=[ANY] * 4,
        out_specs=VMEM,
        scratch_shapes=scratch,
        compiler_params=pltpu.CompilerParams(
            collective_id=0, has_side_effects=True, vmem_limit_bytes=VMEM_LIMIT
        ),
        name="gossip_step",
    )(*args)
    shape = jax.ShapeDtypeStruct((depth, units), BF16)
    outs = pl.pallas_call(
        place_kernel,
        out_shape=[shape, shape],
        in_specs=[VMEM],
        out_specs=[ANY] * 2,
        scratch_shapes=[dma((slabs, 2))],
        compiler_params=pltpu.CompilerParams(vmem_limit_bytes=8 * 1024 * 1024),
        name="place",
    )(pltpu.with_memory_space_constraint(mixed, pltpu.VMEM))
    return tuple(out[None] for out in outs)


def solution(mesh):
    in_specs = (
        P("grp", "dp", None),
        P("grp", "dp", None),
        P("grp", None, "dp"),
        P("grp", None, "dp"),
    )
    out_specs = (P("grp", None, "dp"), P("grp", None, "dp"))
    return jax.shard_map(local, mesh=mesh, in_specs=in_specs, out_specs=out_specs, check_vma=False)
```

time: 183 us -> 158 us (0.86); the launches traced: 183 us -> 155 us
  Pallas kernels: 177 us -> 155 us
  local copies, waits for them, and re-layouts: 5.57 us -> 0 us
    pallas_call x1 -> x2, Pallas kernels: 177 us -> 155 us  [the longest x1 152 us: local(): pl.pallas_call(functools.partial(kernel, n, groups), out_shape=pltpu.VMEM...]
    unnamed x4 -> x0, local copies, waits for them, and re-layouts: 5.57 us -> none
where the time goes in v1:
time: 158 us; the launch traced here: 155 us
  Pallas kernels  155 us (98%)
    pallas_call x1, Pallas kernels, local(): pl.pallas_call(functools.partial(kernel, n, groups), out_shape=pltpu.VMEM...  152 us

profile of v1, /device:TPU:6, one launch (start us, length us, event | category | flops | bytes accessed | tf_op | source)
XLA Modules:
  0.0 155.4 jit_solution(508858954529659429)
XLA Ops:
  0.6 152.1 %gossip_step.1.mixed = bf16[3,2,2048,256]{3,2,1,0:T(8,128)(2,1)S(1)} custom-call(bf16[128,2048]{1,0:T(8,128)(2,1)} %bitcast.9, bf16[128,6144]{1,0:T(8,128)(2,1)} %bitcast.8, bf16[2048,768]{1,0:T(8,128)(2,1)} %bitcast.6, bf16[2048,768]{1,0:T(8,128)(2,1)} %bitcast.7), custom_call_target="tpu_custom_call" | custom-call | tf_op jit(solution)/shard_map/gossip_step/pallas_call | solution.py:423
  152.7 2.7 %place.1 = (bf16[2048,768]{1,0:T(8,128)(2,1)}, bf16[2048,768]{1,0:T(8,128)(2,1)}) custom-call(bf16[3,2,2048,256]{3,2,1,0:T(8,128)(2,1)S(1)} %gossip_step.1.mixed), custom_call_target="tpu_custom_call" | custom-call | tf_op jit(solution)/shard_map/place/pallas_call | solution.py:435

commit v2 on v1

--- a/solution.py
+++ b/solution.py
@@ -32,11 +32,9 @@
 def kernel(n, groups, *refs):
     tokens, hidden, w_gate, w_up, far = refs[:5]
     tok, tok_t, cot, held, near, far_tok, far_tok_t, far_cot, stage, gate_rows, up_rows, gate_pre, up_pre = refs[5:18]
-    local_sem, weight_sem, turn_sem = refs[18:21]
-    gather_sems, far_gather_sems = refs[21:27], refs[27:33]
-    cot_sems, far_cot_sems, early_sems, early_cot_sems, near_sems, far_sems = (
-        refs[k : k + 2] for k in range(33, 45, 2)
-    )
+    local_sem, turn_sem = refs[18:20]
+    gather_sems, far_gather_sems = refs[20:24], refs[24:28]
+    cot_sems, far_cot_sems, early_sems, near_sems, far_sems = (refs[k : k + 2] for k in range(28, 38, 2))
     nx = inner_size(n)
     nz = n // nx
     rows, depth = tokens.shape
@@ -55,16 +53,17 @@
     def hidden_part(to, h):
         return hidden.at[:, pl.ds(pl.multiple_of(to * units + h * width, LANES), width)]
 
-    mine = [pltpu.make_async_copy(tokens, tok.at[aligned(me, rows), :], local_sem.at[slabs])]
+    mine = [pltpu.make_async_copy(tokens, tok.at[aligned(me, rows), :], local_sem.at[0])]
     for h in range(slabs):
-        mine.append(pltpu.make_async_copy(hidden_part(me, h), cot.at[h, aligned(me, rows), :], local_sem.at[h]))
-    for h in range(slabs):
+        mine.append(pltpu.make_async_copy(hidden_part(me, h), cot.at[h, aligned(me, rows), :], local_sem.at[1]))
         for s, w in enumerate((w_gate, w_up)):
-            mine.append(
-                pltpu.make_async_copy(w.at[:, pl.ds(h * width, width)], held.at[h, s], weight_sem.at[h, s])
-            )
+            mine.append(pltpu.make_async_copy(w.at[:, pl.ds(h * width, width)], held.at[h, s], local_sem.at[2]))
     for copy in mine:
         copy.start()
+
+    def wait_mine(k):
+        place = (tok.at[aligned(me, rows), :], cot.at[:, aligned(me, rows), :], held)[k]
+        pltpu.make_async_copy(place, place, local_sem.at[k]).wait()
 
     with jax.named_scope("barrier"):
         barrier = pltpu.get_barrier_semaphore()
@@ -85,50 +84,41 @@
             src_ref=src, dst_ref=dst, send_sem=send, recv_sem=recv, device_id=to, device_id_type=MESH
         )
 
-    def early_tokens():
-        return remote(tokens, far_tok.at[aligned(me, rows), :], early_sems[0].at[0], early_sems[1].at[0], grp=far_grp)
-
-    def early_weights(s):
-        return remote(
-            (w_gate, w_up)[s].at[:, :width], far.at[0, s], early_sems[0].at[1 + s], early_sems[1].at[1 + s], grp=far_grp
-        )
-
-    def early_cot(j, own):
-        place = far_cot.at[aligned(me, rows), :] if own else stage.at[:, aligned(j, width)]
-        return remote(hidden_part(j, 0), place, early_cot_sems[0].at[j], early_cot_sems[1].at[j], grp=far_grp)
-
-    def early():
-        copies = [early_tokens(), early_weights(0), early_weights(1)]
-        copies += [early_cot(lax.rem(me + j, n), False) for j in range(1, n)]
-        return copies + [early_cot(me, True)]
+    def early(k, src, dst):
+        return remote(src, dst, early_sems[0].at[k], early_sems[1].at[k], grp=far_grp)
+
+    def start_early():
+        early(0, tokens, far_tok.at[aligned(me, rows), :]).start()
+        for s, w in enumerate((w_gate, w_up)):
+            early(1, w.at[:, :width], far.at[0, s]).start()
+        for j in range(1, n):
+            to = lax.rem(me + j, n)
+            early(2, hidden_part(to, 0), stage.at[:, aligned(to, width)]).start()
+        early(2, hidden_part(me, 0), far_cot.at[0, aligned(me, rows), :]).start()
+
+    def early_whole():
+        return [early(k, ref, ref) for k, ref in enumerate((far_tok.at[aligned(me, rows), :], far.at[0], stage))]
 
     def relay(buf, sems):
-        up_send, up_recv, down_send, down_recv, side_send, side_recv = sems
+        along_send, along_recv, side_send, side_recv = sems
         piece = rows // PIECES
 
         def slot(zz, xx, c):
             return buf.at[aligned((zz * nx + xx) * PIECES + c, piece), :]
 
-        def along(zz, c, pair, to):
+        def along(zz, c, to):
             place = slot(zz, x, c)
-            return remote(place, place, pair[0].at[zz, c], pair[1].at[zz, c], dp=to * nx + x)
+            return remote(place, place, along_send, along_recv.at[zz, c], dp=to * nx + x)
 
         def up(zz, c, back=False):
-            return along(zz, c, (up_send, up_recv), z - 1 if back else z + 1)
+            return along(zz, c, z - 1 if back else z + 1)
 
         def down(zz, c, back=False):
-            return along(zz, c, (down_send, down_recv), z + 1 if back else z - 1)
+            return along(zz, c, z + 1 if back else z - 1)
 
         def side(zz, j, c):
             place = slot(zz, x, c)
-            return remote(
-                place, place, side_send.at[zz, j - 1, c], side_recv.at[zz, j - 1, c], dp=z * nx + lax.rem(x + j, nx)
-            )
-
-        def side_arrival(zz, j, c):
-            other = lax.rem(x + nx - j, nx)
-            place = slot(zz, other, c)
-            return remote(place, place, side_send.at[zz, j - 1, c], side_recv.at[zz, j - 1, c], dp=z * nx + other)
+            return remote(place, place, side_send, side_recv.at[zz, j - 1], dp=z * nx + lax.rem(x + j, nx))
 
         def pass_on(zz, c, upward):
             if upward is not False:
@@ -161,42 +151,44 @@
 
         def row_ready(zz):
             for j in range(1, nx):
-                for c in range(PIECES):
-                    side_arrival(zz, j, c).wait_recv()
+                other = lax.rem(x + nx - j, nx)
+                place = buf.at[aligned(zz * nx + other, rows), :]
+                remote(place, place, side_send, side_recv.at[zz, j - 1], dp=z * nx + other).wait_recv()
 
         def settle():
-            @pl.loop(0, nz)
-            def _(zz):
-                for c in range(PIECES):
-                    for j in range(1, nx):
-                        side(zz, j, c).wait_send()
-                    pl.when((z + 1 < nz) & (zz <= z))(lambda: up(zz, c).wait_send())
-                    pl.when((z >= 1) & (zz >= z))(lambda: down(zz, c).wait_send())
+            def sent(count, sem):
+                place = buf.at[: count * rows, :]
+                remote(place, place, sem, side_recv.at[0, 0], dp=lax.rem(me + 1, n)).wait_send()
+
+            if nx > 1:
+                sent(nz * (nx - 1), side_send)
+            for at in range(nz):
+                count = (at + 1 if at + 1 < nz else 0) + (nz - at if at >= 1 else 0)
+                if count > 0:
+                    pl.when(z == at)(lambda count=count: sent(count, along_send))
 
         return begin, turn, row_ready, settle
 
-    def swap(block_of, buf_of, sems):
-        def send(to, h):
-            return remote(block_of(to, h), buf_of(h).at[aligned(me, rows), :], sems[0].at[h, to], sems[1].at[h, me], dp=to)
-
-        def arrival(source, h):
-            place = buf_of(h).at[aligned(source, rows), :]
-            return remote(place, place, sems[0].at[h, source], sems[1].at[h, source], dp=source)
-
+    def swap(block_of, buf, sems):
         def send_row(zz, h):
             for xx in range(nx):
-                pl.when(zz * nx + xx != me)(lambda: send(zz * nx + xx, h).start())
-
-        def row_ready(zz, h):
-            for xx in range(nx):
-                pl.when(zz * nx + xx != me)(lambda: arrival(zz * nx + xx, h).wait_recv())
-
-        def settle(h):
-            @pl.loop(0, n)
-            def _(j):
-                pl.when(j != me)(lambda: arrival(j, h).wait_send())
-
-        return send_row, row_ready, settle
+                to = zz * nx + xx
+
+                @pl.when(to != me)
+                def _():
+                    remote(
+                        block_of(to, h), buf.at[h, aligned(me, rows), :], sems[0].at[0], sems[1].at[h], dp=to
+                    ).start()
+
+        def ready(h):
+            place = buf.at[h, : (n - 1) * rows, :]
+            remote(place, place, sems[0].at[0], sems[1].at[h], dp=lax.rem(me + 1, n)).wait_recv()
+
+        def settle():
+            place = buf.at[:, : (n - 1) * rows, :]
+            remote(place, place, sems[0].at[0], sems[1].at[0], dp=lax.rem(me + 1, n)).wait_send()
+
+        return send_row, ready, settle
 
     least = jnp.minimum(z, nz - 1 - z)
     longer = jnp.where(z < nz - 1 - z, 1, -1)
@@ -233,11 +225,22 @@
 
     def near_copy(h, i):
         place = (h, slice(None), aligned(i, BLOCK))
-        return remote(held.at[place], near.at[place], near_sems[0].at[h, i], near_sems[1].at[h, i], grp=near_grp)
+        return remote(held.at[place], near.at[place], near_sems[0].at[0], near_sems[1].at[h], grp=near_grp)
+
+    def near_slab(h):
+        return remote(held.at[h], near.at[h], near_sems[0].at[0], near_sems[1].at[h], grp=near_grp)
 
     def far_copy(h, i):
         place = (h, slice(None), aligned(i, BLOCK))
-        return remote(held.at[place], far.at[place], far_sems[0].at[h, i], far_sems[1].at[h, i], grp=far_grp)
+        k = jnp.where(h == slabs - 1, h + i, h)
+        return remote(held.at[place], far.at[place], far_sems[0].at[0], far_sems[1].at[k], grp=far_grp)
+
+    def far_slab(h):
+        return remote(held.at[h], far.at[h], far_sems[0].at[0], far_sems[1].at[h], grp=far_grp)
+
+    def far_sent(first):
+        place = pl.ds(first, slabs - first)
+        remote(held.at[place], far.at[place], far_sems[0].at[0], far_sems[1].at[0], grp=far_grp).wait_send()
 
     def send_steps(h, i):
         pl.when(even | (h > 0))(lambda: far_copy(h, i).start())
@@ -245,17 +248,17 @@
 
     @pl.when(odd)
     def _():
-        for copy in early():
-            copy.start()
+        start_early()
         with jax.named_scope("wait_turn"):
             pl.semaphore_wait(turn_sem, 1)
 
     begin, turn, tokens_ready, settle_tokens = relay(tok, gather_sems)
-    send_cot, cot_ready, settle_cot = swap(hidden_part, lambda h: cot.at[h], cot_sems)
-    for copy in mine:
-        copy.wait()
+    send_cot, cot_ready, settle_cot = swap(hidden_part, cot, cot_sems)
+    wait_mine(0)
     begin()
     send_cot(z, 0)
+    wait_mine(1)
+    wait_mine(2)
 
     @pl.loop(0, nz)
     def _(r):
@@ -281,11 +284,11 @@
             def _(zz):
                 project(tok, held[h, 0], held[h, 1], zz)
 
+        with jax.named_scope("wait_cot"):
+            cot_ready(h)
+
         @pl.loop(0, nz)
-        def _(r):
-            zz = arriving(r)
-            with jax.named_scope("wait_cot"):
-                cot_ready(zz, h)
+        def _(zz):
             with jax.named_scope("forward"):
                 activate(cot.at[h], zz)
 
@@ -304,12 +307,12 @@
     @pl.when(even)
     def _():
         with jax.named_scope("wait_sibling"):
-            near_copy(0, 0).wait_recv()
-        for copy in early():
+            near_slab(0).wait_recv()
+        for copy in early_whole():
             copy.wait_recv()
         begin, turn, tokens_ready, settle_far_tokens = relay(far_tok, far_gather_sems)
         send_cot, cot_ready, settle_far_cot = swap(
-            lambda to, h: stage.at[:, aligned(to, width)], lambda h: far_cot, far_cot_sems
+            lambda to, h: stage.at[:, aligned(to, width)], far_cot, far_cot_sems
         )
         begin()
 
@@ -327,11 +330,12 @@
                 turn_over(far_tok, far_tok_t, zz)
                 project(far_tok, far[0, 0], far[0, 1], zz)
 
+        with jax.named_scope("wait_cot"):
+            cot_ready(0)
+
         @pl.loop(0, nz)
         def _(zz):
-            with jax.named_scope("wait_cot"):
-                cot_ready(zz, 0)
-            activate(far_cot, zz)
+            activate(far_cot.at[0], zz)
 
         @pl.loop(0, blocks)
         def _(i):
@@ -339,27 +343,31 @@
                 update(far_tok_t, far, 0, i)
 
         settle_far_tokens()
-        settle_far_cot(0)
+        settle_far_cot()
 
     settle_tokens()
-    for h in range(slabs):
-        settle_cot(h)
+    settle_cot()
 
     @pl.when(odd)
     def _():
-        for copy in early():
+        for copy in early_whole():
             copy.wait_send()
 
     @pl.loop(0, slabs)
     def _(h):
+        with jax.named_scope("wait_near"):
+            pl.when(odd | (h > 0))(lambda: near_slab(h).wait_recv())
+        pl.when((h < slabs - 1) & (odd | (h > 0)))(lambda: far_slab(h).wait_recv())
+
+        @pl.when(h == slabs - 1)
+        def _():
+            remote(held, near, near_sems[0].at[0], near_sems[1].at[0], grp=near_grp).wait_send()
+            pl.when(even)(lambda: far_sent(0))
+
         @pl.loop(0, blocks)
         def _(i):
-            near_copy(h, i).wait_send()
-            pl.when(even | (h > 0))(lambda: far_copy(h, i).wait_send())
-            with jax.named_scope("wait_near"):
-                pl.when(odd | (h > 0) | (i > 0))(lambda: near_copy(h, i).wait_recv())
             with jax.named_scope("wait_far"):
-                pl.when(odd | (h > 0))(lambda: far_copy(h, i).wait_recv())
+                pl.when(h == slabs - 1)(lambda: far_copy(h, i).wait_recv())
             with jax.named_scope("mix"):
                 part = aligned(i, BLOCK)
                 for s in range(2):
@@ -367,6 +375,8 @@
                         near[h, s, part, :].astype(F32) + far[h, s, part, :].astype(F32)
                     )
                     far[h, s, part, :] = mixed.astype(BF16)
+
+    pl.when(odd)(lambda: far_sent(1))
 
 
 def place_kernel(mixed, out_gate, out_up, sems):
@@ -394,7 +404,7 @@
     width = units // slabs
     blocks = depth // BLOCK
     dma = pltpu.SemaphoreType.DMA
-    hops = [dma((nz, PIECES))] * 4 + [dma((nz, max(nx - 1, 1), PIECES))] * 2
+    hops = [dma, dma((nz, PIECES)), dma, dma((nz, max(nx - 1, 1)))]
     weights = (slabs, 2, depth, width)
     scratch = [
         pltpu.VMEM((total, depth), BF16),
@@ -404,21 +414,20 @@
         pltpu.VMEM(weights, BF16),
         pltpu.VMEM((total, depth), BF16),
         pltpu.VMEM((depth, total), BF16),
-        pltpu.VMEM((total, width), BF16),
+        pltpu.VMEM((1, total, width), BF16),
         pltpu.VMEM((rows, n * width), BF16),
         pltpu.VMEM((total, width), BF16),
         pltpu.VMEM((total, width), BF16),
         pltpu.VMEM((total, width), F32),
         pltpu.VMEM((total, width), F32),
-        dma((slabs + 1,)), dma((slabs, 2)), pltpu.SemaphoreType.REGULAR,
+        dma((3,)), pltpu.SemaphoreType.REGULAR,
         *hops,
         *hops,
-        dma((slabs, n)), dma((slabs, n)),
-        dma((1, n)), dma((1, n)),
+        dma((1,)), dma((slabs,)),
+        dma((1,)), dma((1,)),
         dma((3,)), dma((3,)),
-        dma((n,)), dma((n,)),
-        dma((slabs, blocks)), dma((slabs, blocks)),
-        dma((slabs, blocks)), dma((slabs, blocks)),
+        dma((1,)), dma((slabs,)),
+        dma((1,)), dma((slabs - 1 + blocks,)),
     ]
     mixed = pl.pallas_call(
         functools.partial(kernel, n, groups),

time: 158 us -> 155 us (0.981)
  Pallas kernels: 155 us -> 153 us
    pallas_call x1, Pallas kernels: 152 us -> 150 us  [local(): pl.pallas_call(functools.partial(kernel, n, groups), out_shape=pltpu.VMEM...]
where the time goes in v2:
time: 155 us; the launch traced here: 153 us
  Pallas kernels  153 us (99%)
    pallas_call x1, Pallas kernels, local(): pl.pallas_call(functools.partial(kernel, n, groups), out_shape=pltpu.VMEM...  150 us

profile of v2, /device:TPU:6, one launch (start us, length us, event | category | flops | bytes accessed | tf_op | source)
XLA Modules:
  0.0 153.4 jit_solution(9886219979120457271)
XLA Ops:
  0.6 150.0 %gossip_step.1.mixed = bf16[3,2,2048,256]{3,2,1,0:T(8,128)(2,1)S(1)} custom-call(bf16[128,2048]{1,0:T(8,128)(2,1)} %bitcast.9, bf16[128,6144]{1,0:T(8,128)(2,1)} %bitcast.8, bf16[2048,768]{1,0:T(8,128)(2,1)} %bitcast.6, bf16[2048,768]{1,0:T(8,128)(2,1)} %bitcast.7), custom_call_target="tpu_custom_call" | custom-call | tf_op jit(solution)/shard_map/gossip_step/pallas_call | solution.py:432
  150.6 2.7 %place.1 = (bf16[2048,768]{1,0:T(8,128)(2,1)}, bf16[2048,768]{1,0:T(8,128)(2,1)}) custom-call(bf16[3,2,2048,256]{3,2,1,0:T(8,128)(2,1)S(1)} %gossip_step.1.mixed), custom_call_target="tpu_custom_call" | custom-call | tf_op jit(solution)/shard_map/place/pallas_call | solution.py:444

commit v3 on v2

--- a/solution.py
+++ b/solution.py
@@ -71,13 +71,20 @@
         def greet(**to):
             pl.semaphore_signal(barrier, inc=1, device_id=to, device_id_type=MESH)
 
-        for j in range(1, nx):
-            greet(dp=z * nx + lax.rem(x + j, nx))
-        pl.when(z >= 1)(lambda: greet(dp=me - nx))
-        pl.when(z + 1 < nz)(lambda: greet(dp=me + nx))
-        greet(grp=near_grp)
         greet(grp=far_grp)
-        pl.semaphore_wait(barrier, nx + 1 + jnp.where(z >= 1, 1, 0) + jnp.where(z + 1 < nz, 1, 0))
+
+        @pl.when(odd)
+        def _():
+            greet(grp=near_grp)
+            pl.semaphore_wait(barrier, 1)
+
+        @pl.when(even)
+        def _():
+            for j in range(1, nx):
+                greet(dp=z * nx + lax.rem(x + j, nx))
+            pl.when(z >= 1)(lambda: greet(dp=me - nx))
+            pl.when(z + 1 < nz)(lambda: greet(dp=me + nx))
+            pl.semaphore_wait(barrier, nx + 1 + jnp.where(z >= 1, 1, 0) + jnp.where(z + 1 < nz, 1, 0))
 
     def remote(src, dst, send, recv, **to):
         return pltpu.make_async_remote_copy(

time: 155 us -> 155 us (level)
  no operation moved by 1% of the time
where the time goes in v3:
time: 155 us; the launch traced here: 153 us
  Pallas kernels  153 us (99%)
    pallas_call x1, Pallas kernels, local(): pl.pallas_call(functools.partial(kernel, n, groups), out_shape=pltpu.VMEM...  150 us

profile of v3, /device:TPU:6, one launch (start us, length us, event | category | flops | bytes accessed | tf_op | source)
XLA Modules:
  0.0 153.3 jit_solution(5479566523679539948)
XLA Ops:
  0.6 150.0 %gossip_step.1.mixed = bf16[3,2,2048,256]{3,2,1,0:T(8,128)(2,1)S(1)} custom-call(bf16[128,2048]{1,0:T(8,128)(2,1)} %bitcast.9, bf16[128,6144]{1,0:T(8,128)(2,1)} %bitcast.8, bf16[2048,768]{1,0:T(8,128)(2,1)} %bitcast.6, bf16[2048,768]{1,0:T(8,128)(2,1)} %bitcast.7), custom_call_target="tpu_custom_call" | custom-call | tf_op jit(solution)/shard_map/gossip_step/pallas_call | solution.py:439
  150.6 2.7 %place.1 = (bf16[2048,768]{1,0:T(8,128)(2,1)}, bf16[2048,768]{1,0:T(8,128)(2,1)}) custom-call(bf16[3,2,2048,256]{3,2,1,0:T(8,128)(2,1)S(1)} %gossip_step.1.mixed), custom_call_target="tpu_custom_call" | custom-call | tf_op jit(solution)/shard_map/place/pallas_call | solution.py:451

commit v4 on v2

--- a/solution.py
+++ b/solution.py
@@ -10,6 +10,7 @@
 LANES = 128
 BLOCK = 256
 PIECES = 2
+WRITES = 4
 VMEM_LIMIT = 54 * 1024 * 1024
 VMEM = pl.BlockSpec(memory_space=pltpu.VMEM)
 ANY = pl.BlockSpec(memory_space=pl.ANY)
@@ -33,8 +34,8 @@
     tokens, hidden, w_gate, w_up, far = refs[:5]
     tok, tok_t, cot, held, near, far_tok, far_tok_t, far_cot, stage, gate_rows, up_rows, gate_pre, up_pre = refs[5:18]
     local_sem, turn_sem = refs[18:20]
-    gather_sems, far_gather_sems = refs[20:24], refs[24:28]
-    cot_sems, far_cot_sems, early_sems, near_sems, far_sems = (refs[k : k + 2] for k in range(28, 38, 2))
+    gather_sems = refs[20:24]
+    cot_sems, early_sems, near_sems, far_sems = (refs[k : k + 2] for k in range(24, 32, 2))
     nx = inner_size(n)
     nz = n // nx
     rows, depth = tokens.shape
@@ -53,6 +54,25 @@
     def hidden_part(to, h):
         return hidden.at[:, pl.ds(pl.multiple_of(to * units + h * width, LANES), width)]
 
+    def wait_mine(k):
+        place = (tok.at[aligned(me, rows), :], cot.at[:, aligned(me, rows), :], held)[k]
+        pltpu.make_async_copy(place, place, local_sem.at[k]).wait()
+
+    barrier = pltpu.get_barrier_semaphore()
+
+    def greet(**to):
+        pl.semaphore_signal(barrier, inc=1, device_id=to, device_id_type=MESH)
+
+    greet(grp=far_grp)
+    pl.when(odd)(lambda: greet(grp=near_grp))
+
+    @pl.when(even)
+    def _():
+        for j in range(1, nx):
+            greet(dp=z * nx + lax.rem(x + j, nx))
+        pl.when(z >= 1)(lambda: greet(dp=me - nx))
+        pl.when(z + 1 < nz)(lambda: greet(dp=me + nx))
+
     mine = [pltpu.make_async_copy(tokens, tok.at[aligned(me, rows), :], local_sem.at[0])]
     for h in range(slabs):
         mine.append(pltpu.make_async_copy(hidden_part(me, h), cot.at[h, aligned(me, rows), :], local_sem.at[1]))
@@ -61,23 +81,9 @@
     for copy in mine:
         copy.start()
 
-    def wait_mine(k):
-        place = (tok.at[aligned(me, rows), :], cot.at[:, aligned(me, rows), :], held)[k]
-        pltpu.make_async_copy(place, place, local_sem.at[k]).wait()
-
     with jax.named_scope("barrier"):
-        barrier = pltpu.get_barrier_semaphore()
-
-        def greet(**to):
-            pl.semaphore_signal(barrier, inc=1, device_id=to, device_id_type=MESH)
-
-        for j in range(1, nx):
-            greet(dp=z * nx + lax.rem(x + j, nx))
-        pl.when(z >= 1)(lambda: greet(dp=me - nx))
-        pl.when(z + 1 < nz)(lambda: greet(dp=me + nx))
-        greet(grp=near_grp)
-        greet(grp=far_grp)
-        pl.semaphore_wait(barrier, nx + 1 + jnp.where(z >= 1, 1, 0) + jnp.where(z + 1 < nz, 1, 0))
+        expected = nx + 1 + jnp.where(z >= 1, 1, 0) + jnp.where(z + 1 < nz, 1, 0)
+        pl.semaphore_wait(barrier, jnp.where(odd, 1, expected))
 
     def remote(src, dst, send, recv, **to):
         return pltpu.make_async_remote_copy(
@@ -88,7 +94,8 @@
         return remote(src, dst, early_sems[0].at[k], early_sems[1].at[k], grp=far_grp)
 
     def start_early():
-        early(0, tokens, far_tok.at[aligned(me, rows), :]).start()
+        place = aligned(me, rows)
+        early(0, tokens, far_tok.at[place, :]).start()
         for s, w in enumerate((w_gate, w_up)):
             early(1, w.at[:, :width], far.at[0, s]).start()
         for j in range(1, n):
@@ -242,8 +249,11 @@
         place = pl.ds(first, slabs - first)
         remote(held.at[place], far.at[place], far_sems[0].at[0], far_sems[1].at[0], grp=far_grp).wait_send()
 
+    late = even & (lax.rem(grp // 2, 2) == 1)
+
     def send_steps(h, i):
-        pl.when(even | (h > 0))(lambda: far_copy(h, i).start())
+        kept = late & (h == slabs - 1) & (i >= blocks // 2)
+        pl.when((even & jnp.logical_not(kept)) | (odd & (h > 0)))(lambda: far_copy(h, i).start())
         near_copy(h, i).start()
 
     @pl.when(odd)
@@ -304,15 +314,18 @@
 
         send_steps(h, blocks - 1)
 
+    settle_tokens()
+    settle_cot()
+
     @pl.when(even)
     def _():
         with jax.named_scope("wait_sibling"):
             near_slab(0).wait_recv()
         for copy in early_whole():
             copy.wait_recv()
-        begin, turn, tokens_ready, settle_far_tokens = relay(far_tok, far_gather_sems)
+        begin, turn, tokens_ready, settle_far_tokens = relay(far_tok, gather_sems)
         send_cot, cot_ready, settle_far_cot = swap(
-            lambda to, h: stage.at[:, aligned(to, width)], far_cot, far_cot_sems
+            lambda to, h: stage.at[:, aligned(to, width)], far_cot, cot_sems
         )
         begin()
 
@@ -345,9 +358,6 @@
         settle_far_tokens()
         settle_far_cot()
 
-    settle_tokens()
-    settle_cot()
-
     @pl.when(odd)
     def _():
         for copy in early_whole():
@@ -362,12 +372,13 @@
         @pl.when(h == slabs - 1)
         def _():
             remote(held, near, near_sems[0].at[0], near_sems[1].at[0], grp=near_grp).wait_send()
-            pl.when(even)(lambda: far_sent(0))
 
         @pl.loop(0, blocks)
         def _(i):
             with jax.named_scope("wait_far"):
                 pl.when(h == slabs - 1)(lambda: far_copy(h, i).wait_recv())
+            freed = i + blocks // 2 - 1
+            pl.when(late & (h == slabs - 1) & (i >= 1) & (freed < blocks))(lambda: far_copy(h, freed).start())
             with jax.named_scope("mix"):
                 part = aligned(i, BLOCK)
                 for s in range(2):
@@ -377,19 +388,17 @@
                     far[h, s, part, :] = mixed.astype(BF16)
 
     pl.when(odd)(lambda: far_sent(1))
+    pl.when(even)(lambda: far_sent(0))
 
 
 def place_kernel(mixed, out_gate, out_up, sems):
-    slabs, _, _, width = mixed.shape
-    copies = [
-        pltpu.make_async_copy(mixed.at[h, s], out.at[:, pl.ds(h * width, width)], sems.at[h, s])
-        for h in range(slabs)
-        for s, out in enumerate((out_gate, out_up))
-    ]
-    for copy in copies:
-        copy.start()
-    for copy in copies:
-        copy.wait()
+    slabs, _, depth, width = mixed.shape
+    for part in range(WRITES):
+        rows = pl.ds(part * depth // WRITES, depth // WRITES)
+        for h in range(slabs):
+            for s, out in enumerate((out_gate, out_up)):
+                pltpu.make_async_copy(mixed.at[h, s, rows], out.at[rows, pl.ds(h * width, width)], sems.at[0]).start()
+    pltpu.make_async_copy(mixed, mixed, sems.at[0]).wait()
 
 
 def local(tokens, hidden_grad, w_gate, w_up):
@@ -422,9 +431,7 @@
         pltpu.VMEM((total, width), F32),
         dma((3,)), pltpu.SemaphoreType.REGULAR,
         *hops,
-        *hops,
         dma((1,)), dma((slabs,)),
-        dma((1,)), dma((1,)),
         dma((3,)), dma((3,)),
         dma((1,)), dma((slabs,)),
         dma((1,)), dma((slabs - 1 + blocks,)),
@@ -446,7 +453,7 @@
         out_shape=[shape, shape],
         in_specs=[VMEM],
         out_specs=[ANY] * 2,
-        scratch_shapes=[dma((slabs, 2))],
+        scratch_shapes=[dma((1,))],
         compiler_params=pltpu.CompilerParams(vmem_limit_bytes=8 * 1024 * 1024),
         name="place",
     )(pltpu.with_memory_space_constraint(mixed, pltpu.VMEM))

time: 155 us -> 154 us (level)
  no operation moved by 1% of the time
where the time goes in v4:
time: 154 us; the launch traced here: 153 us
  Pallas kernels  152 us (99%)
    pallas_call x1, Pallas kernels, local(): pl.pallas_call(functools.partial(kernel, n, groups), out_shape=pltpu.VMEM...  150 us

profile of v4, /device:TPU:6, one launch (start us, length us, event | category | flops | bytes accessed | tf_op | source)
XLA Modules:
  0.0 153.1 jit_solution(14708382447106044177)
XLA Ops:
  0.6 149.8 %gossip_step.1.mixed = bf16[3,2,2048,256]{3,2,1,0:T(8,128)(2,1)S(1)} custom-call(bf16[128,2048]{1,0:T(8,128)(2,1)} %bitcast.9, bf16[128,6144]{1,0:T(8,128)(2,1)} %bitcast.8, bf16[2048,768]{1,0:T(8,128)(2,1)} %bitcast.6, bf16[2048,768]{1,0:T(8,128)(2,1)} %bitcast.7), custom_call_target="tpu_custom_call" | custom-call | tf_op jit(solution)/shard_map/gossip_step/pallas_call | solution.py:439
  150.5 2.6 %place.1 = (bf16[2048,768]{1,0:T(8,128)(2,1)}, bf16[2048,768]{1,0:T(8,128)(2,1)}) custom-call(bf16[3,2,2048,256]{3,2,1,0:T(8,128)(2,1)S(1)} %gossip_step.1.mixed), custom_call_target="tpu_custom_call" | custom-call | tf_op jit(solution)/shard_map/place/pallas_call | solution.py:451

commit v5 on v4

--- a/solution.py
+++ b/solution.py
@@ -10,8 +10,9 @@
 LANES = 128
 BLOCK = 256
 PIECES = 2
-WRITES = 4
-VMEM_LIMIT = 54 * 1024 * 1024
+LAG = 2
+VMEM_LIMIT = 42 * 1024 * 1024
+SMALL_LIMIT = 8 * 1024 * 1024
 VMEM = pl.BlockSpec(memory_space=pltpu.VMEM)
 ANY = pl.BlockSpec(memory_space=pl.ANY)
 MESH = pl.DeviceIdType.MESH
@@ -26,13 +27,30 @@
     return next(count for count in (3, 2, 1) if units % (count * LANES) == 0)
 
 
+def closing_rows(depth):
+    return (depth // BLOCK - depth // BLOCK // 2) * BLOCK
+
+
 def aligned(index, size):
     return pl.ds(pl.multiple_of(index * size, size), size)
 
 
+def roles(groups):
+    grp = lax.axis_index("grp")
+    odd = lax.rem(grp, 2) == 1
+    near_grp = jnp.where(odd, grp - 1, grp + 1)
+    far_grp = jnp.where(odd, lax.rem(grp + 1, groups), lax.rem(grp + groups - 1, groups))
+    second = lax.rem(jnp.where(odd, far_grp, grp) // 2, 2) == 1
+    return odd, near_grp, far_grp, second
+
+
+def blend(own, near, far):
+    return (0.5 * own.astype(F32) + 0.25 * (near.astype(F32) + far.astype(F32))).astype(BF16)
+
+
 def kernel(n, groups, *refs):
-    tokens, hidden, w_gate, w_up, far = refs[:5]
-    tok, tok_t, cot, held, near, far_tok, far_tok_t, far_cot, stage, gate_rows, up_rows, gate_pre, up_pre = refs[5:18]
+    tokens, hidden, w_gate, w_up, far, held, near = refs[:7]
+    tok, tok_t, cot, far_tok, far_tok_t, far_cot, stage, gate_rows, up_rows, gate_pre, up_pre = refs[7:18]
     local_sem, turn_sem = refs[18:20]
     gather_sems = refs[20:24]
     cot_sems, early_sems, near_sems, far_sems = (refs[k : k + 2] for k in range(24, 32, 2))
@@ -44,12 +62,10 @@
     scale = depth ** (-0.5)
     blocks = depth // BLOCK
     span = nx * rows
-    grp, me = lax.axis_index("grp"), lax.axis_index("dp")
+    me = lax.axis_index("dp")
     z, x = me // nx, lax.rem(me, nx)
-    odd = lax.rem(grp, 2) == 1
+    odd, near_grp, far_grp, second = roles(groups)
     even = jnp.logical_not(odd)
-    near_grp = jnp.where(odd, grp - 1, grp + 1)
-    far_grp = jnp.where(odd, lax.rem(grp + 1, groups), lax.rem(grp + groups - 1, groups))
 
     def hidden_part(to, h):
         return hidden.at[:, pl.ds(pl.multiple_of(to * units + h * width, LANES), width)]
@@ -240,20 +256,20 @@
     def far_copy(h, i):
         place = (h, slice(None), aligned(i, BLOCK))
         k = jnp.where(h == slabs - 1, h + i, h)
-        return remote(held.at[place], far.at[place], far_sems[0].at[0], far_sems[1].at[k], grp=far_grp)
+        last = jnp.where(h == slabs - 1, 1, 0)
+        return remote(held.at[place], far.at[place], far_sems[0].at[last], far_sems[1].at[k], grp=far_grp)
 
     def far_slab(h):
         return remote(held.at[h], far.at[h], far_sems[0].at[0], far_sems[1].at[h], grp=far_grp)
 
-    def far_sent(first):
-        place = pl.ds(first, slabs - first)
-        remote(held.at[place], far.at[place], far_sems[0].at[0], far_sems[1].at[0], grp=far_grp).wait_send()
-
-    late = even & (lax.rem(grp // 2, 2) == 1)
+    def far_sent(k, place):
+        remote(held.at[place], far.at[place], far_sems[0].at[k], far_sems[1].at[0], grp=far_grp).wait_send()
+
+    kept = blocks // 2
 
     def send_steps(h, i):
-        kept = late & (h == slabs - 1) & (i >= blocks // 2)
-        pl.when((even & jnp.logical_not(kept)) | (odd & (h > 0)))(lambda: far_copy(h, i).start())
+        now = (h < slabs - 1) | (i < kept) | (odd & jnp.logical_not(second))
+        pl.when(now & (even | (h > 0)))(lambda: far_copy(h, i).start())
         near_copy(h, i).start()
 
     @pl.when(odd)
@@ -373,32 +389,100 @@
         def _():
             remote(held, near, near_sems[0].at[0], near_sems[1].at[0], grp=near_grp).wait_send()
 
-        @pl.loop(0, blocks)
+        @pl.loop(0, jnp.where(second & (h == slabs - 1), kept, blocks))
         def _(i):
             with jax.named_scope("wait_far"):
                 pl.when(h == slabs - 1)(lambda: far_copy(h, i).wait_recv())
-            freed = i + blocks // 2 - 1
-            pl.when(late & (h == slabs - 1) & (i >= 1) & (freed < blocks))(lambda: far_copy(h, freed).start())
+            freed = i + kept - LAG
+            behind = even & jnp.logical_not(second) & (h == slabs - 1)
+            pl.when(behind & (freed >= kept) & (freed < blocks))(lambda: far_copy(h, freed).start())
             with jax.named_scope("mix"):
                 part = aligned(i, BLOCK)
                 for s in range(2):
-                    mixed = 0.5 * held[h, s, part, :].astype(F32) + 0.25 * (
-                        near[h, s, part, :].astype(F32) + far[h, s, part, :].astype(F32)
-                    )
-                    far[h, s, part, :] = mixed.astype(BF16)
-
-    pl.when(odd)(lambda: far_sent(1))
-    pl.when(even)(lambda: far_sent(0))
+                    far[h, s, part, :] = blend(held[h, s, part, :], near[h, s, part, :], far[h, s, part, :])
+
+    pl.when(odd)(lambda: far_sent(0, pl.ds(1, slabs - 2)))
+    pl.when(even)(lambda: far_sent(0, pl.ds(0, slabs - 1)))
+    pl.when(second)(lambda: far_sent(1, (slabs - 1, slice(None), pl.ds(0, kept * BLOCK))))
+    pl.when(jnp.logical_not(second))(lambda: far_sent(1, slabs - 1))
+
+
+def closing_kernel(groups, mixed, held, near, placed, tail, send_sem, recv_sem):
+    _, _, far_grp, second = roles(groups)
+    last = held.shape[0] - 1
+    depth = tail.shape[1]
+    start = held.shape[2] - depth
+
+    @pl.when(second)
+    def _():
+        barrier = pltpu.get_barrier_semaphore()
+        pl.semaphore_signal(barrier, inc=1, device_id={"grp": far_grp}, device_id_type=MESH)
+        pl.semaphore_wait(barrier, 1)
+
+        def copy(i):
+            return pltpu.make_async_remote_copy(
+                src_ref=held.at[last, :, pl.ds(pl.multiple_of(start + i * BLOCK, BLOCK), BLOCK)],
+                dst_ref=tail.at[:, aligned(i, BLOCK)], send_sem=send_sem.at[0], recv_sem=recv_sem.at[i],
+                device_id={"grp": far_grp}, device_id_type=MESH,
+            )
+
+        @pl.loop(0, depth // BLOCK)
+        def _(i):
+            copy(i).start()
+
+        @pl.loop(0, depth // BLOCK)
+        def _(i):
+            with jax.named_scope("wait_tail"):
+                copy(i).wait_recv()
+            part = aligned(i, BLOCK)
+            rows = pl.ds(pl.multiple_of(start + i * BLOCK, BLOCK), BLOCK)
+            for s in range(2):
+                tail[s, part, :] = blend(held[last, s, rows, :], near[last, s, rows, :], tail[s, part, :])
+
+        pltpu.make_async_remote_copy(
+            src_ref=tail, dst_ref=tail, send_sem=send_sem.at[0], recv_sem=recv_sem.at[0],
+            device_id={"grp": far_grp}, device_id_type=MESH,
+        ).wait_send()
+
+    @pl.when(jnp.logical_not(second))
+    def _():
+        for s in range(2):
+            tail[s] = mixed[last, s, start:, :]
 
 
 def place_kernel(mixed, out_gate, out_up, sems):
     slabs, _, depth, width = mixed.shape
-    for part in range(WRITES):
-        rows = pl.ds(part * depth // WRITES, depth // WRITES)
-        for h in range(slabs):
+    copies = []
+    for h in range(slabs):
+        step = depth // 4
+        for start in range(0, depth if h < slabs - 1 else depth - closing_rows(depth), step):
             for s, out in enumerate((out_gate, out_up)):
-                pltpu.make_async_copy(mixed.at[h, s, rows], out.at[rows, pl.ds(h * width, width)], sems.at[0]).start()
-    pltpu.make_async_copy(mixed, mixed, sems.at[0]).wait()
+                rows = pl.ds(start, step)
+                copies.append(
+                    pltpu.make_async_copy(mixed.at[h, s, rows], out.at[rows, pl.ds(h * width, width)], sems.at[len(copies)])
+                )
+    for copy in copies:
+        copy.start()
+    for copy in copies:
+        copy.wait()
+
+
+def place_tail_kernel(tail, held_gate, held_up, out_gate, out_up, sems):
+    _, rows, width = tail.shape
+    depth, units = out_gate.shape
+    step = rows // 2
+    copies = [
+        pltpu.make_async_copy(
+            tail.at[s, pl.ds(k * step, step)],
+            out.at[pl.ds(depth - rows + k * step, step), pl.ds(units - width, width)], sems.at[s, k],
+        )
+        for s, out in enumerate((out_gate, out_up))
+        for k in range(2)
+    ]
+    for copy in copies:
+        copy.start()
+    for copy in copies:
+        copy.wait()
 
 
 def local(tokens, hidden_grad, w_gate, w_up):
@@ -419,8 +503,6 @@
         pltpu.VMEM((total, depth), BF16),
         pltpu.VMEM((depth, total), BF16),
         pltpu.VMEM((slabs, total, width), BF16),
-        pltpu.VMEM(weights, BF16),
-        pltpu.VMEM(weights, BF16),
         pltpu.VMEM((total, depth), BF16),
         pltpu.VMEM((depth, total), BF16),
         pltpu.VMEM((1, total, width), BF16),
@@ -434,29 +516,56 @@
         dma((1,)), dma((slabs,)),
         dma((3,)), dma((3,)),
         dma((1,)), dma((slabs,)),
-        dma((1,)), dma((slabs - 1 + blocks,)),
+        dma((2,)), dma((slabs - 1 + blocks,)),
     ]
-    mixed = pl.pallas_call(
+    kept = pltpu.VMEM(weights, BF16)
+    mixed, held, near = pl.pallas_call(
         functools.partial(kernel, n, groups),
-        out_shape=pltpu.VMEM(weights, BF16),
+        out_shape=[kept, kept, kept],
         in_specs=[ANY] * 4,
-        out_specs=VMEM,
+        out_specs=[VMEM] * 3,
         scratch_shapes=scratch,
         compiler_params=pltpu.CompilerParams(
             collective_id=0, has_side_effects=True, vmem_limit_bytes=VMEM_LIMIT
         ),
         name="gossip_step",
     )(*args)
+    mixed, held, near = (pltpu.with_memory_space_constraint(a, pltpu.VMEM) for a in (mixed, held, near))
     shape = jax.ShapeDtypeStruct((depth, units), BF16)
     outs = pl.pallas_call(
         place_kernel,
         out_shape=[shape, shape],
         in_specs=[VMEM],
         out_specs=[ANY] * 2,
-        scratch_shapes=[dma((1,))],
-        compiler_params=pltpu.CompilerParams(vmem_limit_bytes=8 * 1024 * 1024),
+        scratch_shapes=[dma((8 * slabs,))],
+        compiler_params=pltpu.CompilerParams(vmem_limit_bytes=SMALL_LIMIT),
         name="place",
-    )(pltpu.with_memory_space_constraint(mixed, pltpu.VMEM))
+    )(mixed)
+    tail_rows = closing_rows(depth)
+    tail = pl.pallas_call(
+        functools.partial(closing_kernel, groups),
+        out_shape=pltpu.VMEM((2, tail_rows, width), BF16),
+        in_specs=[VMEM] * 3 + [ANY],
+        out_specs=VMEM,
+        scratch_shapes=[dma((1,)), dma((tail_rows // BLOCK,))],
+        compiler_params=pltpu.CompilerParams(
+            collective_id=1, has_side_effects=True, vmem_limit_bytes=SMALL_LIMIT
+        ),
+        name="closing",
+    )(mixed, held, near, pltpu.with_memory_space_constraint(outs[0], pltpu.HBM))
+    outs = pl.pallas_call(
+        place_tail_kernel,
+        out_shape=[shape, shape],
+        in_specs=[VMEM, ANY, ANY],
+        out_specs=[ANY] * 2,
+        input_output_aliases={1: 0, 2: 1},
+        scratch_shapes=[dma((2, 2))],
+        compiler_params=pltpu.CompilerParams(vmem_limit_bytes=SMALL_LIMIT),
+        name="place_tail",
+    )(
+        pltpu.with_memory_space_constraint(tail, pltpu.VMEM),
+        *(pltpu.with_memory_space_constraint(out, pltpu.HBM) for out in outs),
+    )
     return tuple(out[None] for out in outs)
 
 

time: 154 us -> 152 us (0.987)
  Pallas kernels: 152 us -> 150 us
    pallas_call x1 -> x3, Pallas kernels: 150 us -> 148 us  [the longest x1 128 us: local(): pl.pallas_call(functools.partial(kernel, n, groups), out_shape=[kept, kep...]
where the time goes in v5:
time: 152 us; the launch traced here: 151 us
  Pallas kernels  150 us (99%)
    pallas_call x1, Pallas kernels, local(): pl.pallas_call(functools.partial(kernel, n, groups), out_shape=[kept, kep...  128 us
    pallas_call x1, Pallas kernels, local(): pl.pallas_call(functools.partial(closing_kernel, groups), out_shape=pltpu...  18.8 us

profile of v5, /device:TPU:6, one launch (start us, length us, event | category | flops | bytes accessed | tf_op | source)
XLA Modules:
  0.0 151.1 jit_solution(3878651765482366624)
XLA Ops:
  0.6 128.1 %gossip_step.1 = (bf16[3,2,2048,256]{3,2,1,0:T(8,128)(2,1)S(1)}, bf16[3,2,2048,256]{3,2,1,0:T(8,128)(2,1)S(1)}, bf16[3,2,2048,256]{3,2,1,0:T(8,128)(2,1)S(1)}) custom-call(bf16[128,2048]{1,0:T(8,128)(2,1)} %bitcast.11, bf16[128,6144]{1,0:T(8,128)(2,1)} %bitcast.10, bf16[2048,768]{1,0:T(8,128)(2,1)} %bitcast.8, bf16[2048,768]{1,0:T(8,128)(2,1)} %bitcast.9), custom_call_target="tpu_custom_call" | custom-call | tf_op jit(solution)/shard_map/gossip_step/pallas_call | solution.py:522
  128.8 2.5 %place.1 = (bf16[2048,768]{1,0:T(8,128)(2,1)}, bf16[2048,768]{1,0:T(8,128)(2,1)}) custom-call(bf16[3,2,2048,256]{3,2,1,0:T(8,128)(2,1)S(1)} %get-tuple-element.9.mixed), custom_call_target="tpu_custom_call" | custom-call | tf_op jit(solution)/shard_map/place/pallas_call | solution.py:535
  131.3 18.8 %closing.1.tail = bf16[2,1024,256]{2,1,0:T(8,128)(2,1)S(1)} custom-call(bf16[3,2,2048,256]{3,2,1,0:T(8,128)(2,1)S(1)} %get-tuple-element.9.mixed, bf16[3,2,2048,256]{3,2,1,0:T(8,128)(2,1)S(1)} %get-tuple-element.10.held, bf16[3,2,2048,256]{3,2,1,0:T(8,128)(2,1)S(1)} %get-tuple-element.11.near, bf16[2048,768]{1,0:T(8,128)(2,1)} %get-tuple-element.12.placed.held_gate), custom_call_target="tpu_custom_call" | custom-call | tf_op jit(solution)/shard_map/closing/pallas_call | solution.py:545
  150.1 1.0 place_tail.1

commit v6 on v5

--- a/solution.py
+++ b/solution.py
@@ -94,8 +94,7 @@
         mine.append(pltpu.make_async_copy(hidden_part(me, h), cot.at[h, aligned(me, rows), :], local_sem.at[1]))
         for s, w in enumerate((w_gate, w_up)):
             mine.append(pltpu.make_async_copy(w.at[:, pl.ds(h * width, width)], held.at[h, s], local_sem.at[2]))
-    for copy in mine:
-        copy.start()
+    pl.when(even)(lambda: mine[0].start())
 
     with jax.named_scope("barrier"):
         expected = nx + 1 + jnp.where(z >= 1, 1, 0) + jnp.where(z + 1 < nz, 1, 0)
@@ -275,6 +274,7 @@
     @pl.when(odd)
     def _():
         start_early()
+        mine[0].start()
         with jax.named_scope("wait_turn"):
             pl.semaphore_wait(turn_sem, 1)
 
@@ -282,6 +282,8 @@
     send_cot, cot_ready, settle_cot = swap(hidden_part, cot, cot_sems)
     wait_mine(0)
     begin()
+    for copy in mine[1:]:
+        copy.start()
     send_cot(z, 0)
     wait_mine(1)
     wait_mine(2)

time: 152 us -> 152 us (level)
  no operation moved by 1% of the time
where the time goes in v6:
time: 152 us; the launch traced here: 151 us
  Pallas kernels  150 us (99%)
    pallas_call x1, Pallas kernels, local(): pl.pallas_call(functools.partial(kernel, n, groups), out_shape=[kept, kep...  128 us
    pallas_call x1, Pallas kernels, local(): pl.pallas_call(functools.partial(closing_kernel, groups), out_shape=pltpu...  18.8 us

profile of v6, /device:TPU:6, one launch (start us, length us, event | category | flops | bytes accessed | tf_op | source)
XLA Modules:
  0.0 151.1 jit_solution(7798664311856678051)
XLA Ops:
  0.6 128.1 %gossip_step.1 = (bf16[3,2,2048,256]{3,2,1,0:T(8,128)(2,1)S(1)}, bf16[3,2,2048,256]{3,2,1,0:T(8,128)(2,1)S(1)}, bf16[3,2,2048,256]{3,2,1,0:T(8,128)(2,1)S(1)}) custom-call(bf16[128,2048]{1,0:T(8,128)(2,1)} %bitcast.11, bf16[128,6144]{1,0:T(8,128)(2,1)} %bitcast.10, bf16[2048,768]{1,0:T(8,128)(2,1)} %bitcast.8, bf16[2048,768]{1,0:T(8,128)(2,1)} %bitcast.9), custom_call_target="tpu_custom_call" | custom-call | tf_op jit(solution)/shard_map/gossip_step/pallas_call | solution.py:524
  128.8 2.5 %place.1 = (bf16[2048,768]{1,0:T(8,128)(2,1)}, bf16[2048,768]{1,0:T(8,128)(2,1)}) custom-call(bf16[3,2,2048,256]{3,2,1,0:T(8,128)(2,1)S(1)} %get-tuple-element.9.mixed), custom_call_target="tpu_custom_call" | custom-call | tf_op jit(solution)/shard_map/place/pallas_call | solution.py:537
  131.3 18.8 %closing.1.tail = bf16[2,1024,256]{2,1,0:T(8,128)(2,1)S(1)} custom-call(bf16[3,2,2048,256]{3,2,1,0:T(8,128)(2,1)S(1)} %get-tuple-element.9.mixed, bf16[3,2,2048,256]{3,2,1,0:T(8,128)(2,1)S(1)} %get-tuple-element.10.held, bf16[3,2,2048,256]{3,2,1,0:T(8,128)(2,1)S(1)} %get-tuple-element.11.near, bf16[2048,768]{1,0:T(8,128)(2,1)} %get-tuple-element.12.placed.held_gate), custom_call_target="tpu_custom_call" | custom-call | tf_op jit(solution)/shard_map/closing/pallas_call | solution.py:547
  150.1 1.0 place_tail.1

commit v7 on v6

--- a/solution.py
+++ b/solution.py
@@ -10,7 +10,7 @@
 LANES = 128
 BLOCK = 256
 PIECES = 2
-LAG = 2
+LAG = 1
 VMEM_LIMIT = 42 * 1024 * 1024
 SMALL_LIMIT = 8 * 1024 * 1024
 VMEM = pl.BlockSpec(memory_space=pltpu.VMEM)

time: 152 us -> 152 us (level)
  no operation moved by 1% of the time
where the time goes in v7:
time: 152 us; the launch traced here: 151 us
  Pallas kernels  150 us (99%)
    pallas_call x1, Pallas kernels, local(): pl.pallas_call(functools.partial(kernel, n, groups), out_shape=[kept, kep...  129 us
    pallas_call x1, Pallas kernels, local(): pl.pallas_call(functools.partial(closing_kernel, groups), out_shape=pltpu...  17.5 us

profile of v7, /device:TPU:6, one launch (start us, length us, event | category | flops | bytes accessed | tf_op | source)
XLA Modules:
  0.0 151.1 jit_solution(15261885819660726637)
XLA Ops:
  0.6 129.5 %gossip_step.1 = (bf16[3,2,2048,256]{3,2,1,0:T(8,128)(2,1)S(1)}, bf16[3,2,2048,256]{3,2,1,0:T(8,128)(2,1)S(1)}, bf16[3,2,2048,256]{3,2,1,0:T(8,128)(2,1)S(1)}) custom-call(bf16[128,2048]{1,0:T(8,128)(2,1)} %bitcast.11, bf16[128,6144]{1,0:T(8,128)(2,1)} %bitcast.10, bf16[2048,768]{1,0:T(8,128)(2,1)} %bitcast.8, bf16[2048,768]{1,0:T(8,128)(2,1)} %bitcast.9), custom_call_target="tpu_custom_call" | custom-call | tf_op jit(solution)/shard_map/gossip_step/pallas_call | solution.py:524
  130.1 2.5 %place.1 = (bf16[2048,768]{1,0:T(8,128)(2,1)}, bf16[2048,768]{1,0:T(8,128)(2,1)}) custom-call(bf16[3,2,2048,256]{3,2,1,0:T(8,128)(2,1)S(1)} %get-tuple-element.9.mixed), custom_call_target="tpu_custom_call" | custom-call | tf_op jit(solution)/shard_map/place/pallas_call | solution.py:537
  132.7 17.5 %closing.1.tail = bf16[2,1024,256]{2,1,0:T(8,128)(2,1)S(1)} custom-call(bf16[3,2,2048,256]{3,2,1,0:T(8,128)(2,1)S(1)} %get-tuple-element.9.mixed, bf16[3,2,2048,256]{3,2,1,0:T(8,128)(2,1)S(1)} %get-tuple-element.10.held, bf16[3,2,2048,256]{3,2,1,0:T(8,128)(2,1)S(1)} %get-tuple-element.11.near, bf16[2048,768]{1,0:T(8,128)(2,1)} %get-tuple-element.12.placed.held_gate), custom_call_target="tpu_custom_call" | custom-call | tf_op jit(solution)/shard_map/closing/pallas_call | solution.py:547
  150.1 1.0 place_tail.1
